TPU v7x, 32 devices: a whole 2x2x4 slice. The times are simulated.
32 devices in a mesh: cand: 4 (over y, core), tensor: 8 (over z, x).
Axes of the slice: x: 2, y: 2, z: 4, core: 2. Of those that a mesh axis runs over, the one named last changes fastest.
Arguments:
- states: bfloat16 [512, 3584], P('cand'), may hold values from -60 to 60
- targets: int32 [512], replicated, may hold values from 0 to 131071
- loss_mask: int32 [512], P('cand'), may hold values 0 or 1
- cand_of: int32 [4], replicated, may hold values from 0 to 3
- lambdas: float32 [4], replicated, may hold values from 0.2 to 1
- base_q: bfloat16 [3584, 4096], P('cand', 'tensor'), may hold values from -0.09375 to 0.09375
- delta_q: bfloat16 [2, 3584, 4096], P(None, 'cand', 'tensor'), may hold values from -0.046875 to 0.046875
- base_k: bfloat16 [3584, 2048], P('cand'), may hold values from -0.09375 to 0.09375
- delta_k: bfloat16 [2, 3584, 2048], P(None, 'cand'), may hold values from -0.046875 to 0.046875
- base_v: bfloat16 [3584, 2048], P('cand'), may hold values from -0.09375 to 0.09375
- delta_v: bfloat16 [2, 3584, 2048], P(None, 'cand'), may hold values from -0.046875 to 0.046875
- base_o: bfloat16 [4096, 3584], P('tensor', 'cand'), may hold values from -0.09375 to 0.09375
- delta_o: bfloat16 [2, 4096, 3584], P(None, 'tensor', 'cand'), may hold values from -0.046875 to 0.046875
- pre_gain: float32 [3584], replicated, may hold values from 0.5 to 2
- post_gain: float32 [3584], replicated, may hold values from 0.5 to 2
- final_gain: float32 [3584], replicated, may hold values from 0.5 to 2
- unembed: bfloat16 [3584, 131072], P(None, ('cand', 'tensor')), may hold values from -0.3125 to 0.3125
Outputs:
- token_loss: float32 [512], P('cand')
- cand_loss: float32 [4], replicated
All inputs are finite; a program needn't handle non-finite values. No bound on the sum of `loss_mask` on one device may be relied on, other than what follows from the above.
Results may differ from a plain program's by a relative error of at most 0.002.
Values may be sent and summed in bfloat16 or wider, within the bound.
No kernel may reach another device: no remote copies, remote signals or barrier semaphores. Data moves between devices by JAX's collectives and lax.ppermute only.
A program may use at most 128 MiB of HBM per device.

v0:
```python
import math
import jax
import jax.numpy as jnp
from jax import lax
from jax.sharding import PartitionSpec as P

KV = 8
HEAD_SIZE = 256
CANDS = 4


def root_norm(entries, scale_gain):
    mean_square = jnp.mean(entries * entries, axis=-1, keepdims=True)
    return entries * lax.rsqrt(mean_square + 1e-06) * scale_gain


def rotate_pairs(entries, length):
    half_width = entries.shape[-1] // 2
    positions = jnp.arange(length).astype(jnp.float32)
    frequency = jnp.exp(
        -math.log(10000.0) * jnp.arange(half_width).astype(jnp.float32) * 2.0 / entries.shape[-1]
    )
    angles = positions[:, None] * frequency[None, :]
    cosine = jnp.cos(angles)[:, None, :]
    sine_part = jnp.sin(angles)[:, None, :]
    first = entries[..., :half_width]
    second = entries[..., half_width:]
    return jnp.concatenate(
        [first * cosine - second * sine_part, second * cosine + first * sine_part], axis=-1
    )


def task_total(delta):
    return jnp.sum(delta.astype(jnp.float32), axis=0).astype(jnp.bfloat16)


def merge_weights(base, total, mixing):
    return (base.astype(jnp.float32) + mixing * total.astype(jnp.float32)).astype(jnp.bfloat16)


def on_device(
    states,
    targets,
    loss_mask,
    cand_of,
    lambdas,
    base_q,
    delta_q,
    base_k,
    delta_k,
    base_v,
    delta_v,
    base_o,
    delta_o,
    pre_gain,
    post_gain,
    final_gain,
    unembed,
):
    cand_id = lax.axis_index("cand")
    tensor_id = lax.axis_index("tensor")
    tensor_count = lax.axis_size("tensor")
    chosen = cand_of[cand_id]
    mixing = lambdas[chosen]
    group_size = tensor_count // KV
    head_start = tensor_id // group_size * HEAD_SIZE
    own_base_k = lax.dynamic_slice_in_dim(base_k, head_start, HEAD_SIZE, 1)
    own_base_v = lax.dynamic_slice_in_dim(base_v, head_start, HEAD_SIZE, 1)
    own_delta_k = lax.dynamic_slice_in_dim(delta_k, head_start, HEAD_SIZE, 2)
    own_delta_v = lax.dynamic_slice_in_dim(delta_v, head_start, HEAD_SIZE, 2)
    summed = [task_total(delta) for delta in (delta_q, own_delta_k, own_delta_v, delta_o)]
    pieces = (
        lax.all_gather(base_q, "cand", axis=0, tiled=True),
        lax.all_gather(own_base_k, "cand", axis=0, tiled=True),
        lax.all_gather(own_base_v, "cand", axis=0, tiled=True),
        lax.all_gather(base_o, "cand", axis=1, tiled=True),
        lax.all_gather(summed[0], "cand", axis=0, tiled=True),
        lax.all_gather(summed[1], "cand", axis=0, tiled=True),
        lax.all_gather(summed[2], "cand", axis=0, tiled=True),
        lax.all_gather(summed[3], "cand", axis=1, tiled=True),
    )
    base_parts = pieces[:4]
    task_parts = pieces[4:]
    w_query = merge_weights(base_parts[0], task_parts[0], mixing)
    w_key = merge_weights(base_parts[1], task_parts[1], mixing)
    w_value = merge_weights(base_parts[2], task_parts[2], mixing)
    w_out = merge_weights(base_parts[3], task_parts[3], mixing)
    length = states.shape[0]
    stream = states.astype(jnp.float32)
    normed = root_norm(stream, pre_gain).astype(jnp.bfloat16)
    query_rows = jnp.dot(normed, w_query, preferred_element_type=jnp.float32).reshape(
        length, -1, HEAD_SIZE
    )
    query_rows = rotate_pairs(query_rows, length).astype(jnp.bfloat16)
    key_full = jnp.dot(normed, w_key, preferred_element_type=jnp.float32).astype(jnp.bfloat16)
    value_full = jnp.dot(normed, w_value, preferred_element_type=jnp.float32).astype(jnp.bfloat16)
    key_matrix = rotate_pairs(
        key_full.astype(jnp.float32).reshape(length, 1, HEAD_SIZE), length
    ).astype(jnp.bfloat16)[:, 0, :]
    attention_scores = jnp.einsum(
        "lhd,md->hlm", query_rows, key_matrix, preferred_element_type=jnp.float32
    ) * HEAD_SIZE ** (-0.5)
    attention_scores = 50.0 * jnp.tanh(attention_scores / 50.0)
    causal = jnp.arange(length)[:, None] >= jnp.arange(length)[None, :]
    weights = jnp.where(causal[None, :, :], jnp.exp(attention_scores), 0.0)
    attention_probs = (weights / jnp.sum(weights, axis=-1, keepdims=True)).astype(jnp.bfloat16)
    context_rows = jnp.einsum(
        "hlm,md->lhd", attention_probs, value_full, preferred_element_type=jnp.float32
    )
    context_rows = context_rows.astype(jnp.bfloat16).reshape(length, -1)
    partial_value = jnp.dot(context_rows, w_out, preferred_element_type=jnp.float32)
    vocab_width = unembed.shape[1]
    vocab_start = (cand_id * tensor_count + tensor_id) * vocab_width
    vocab_index = jnp.arange(vocab_width)
    attended = lax.psum(partial_value, "tensor")
    final_rows = root_norm(stream + root_norm(attended, post_gain), final_gain).astype(jnp.bfloat16)
    logits = jnp.dot(
        lax.all_gather(final_rows, "cand", axis=0, tiled=True),
        unembed,
        preferred_element_type=jnp.float32,
    )
    capped = 30.0 * jnp.tanh(logits / 30.0)
    totals = jnp.sum(jnp.exp(capped), axis=1)
    local_ids = targets - vocab_start
    matches = local_ids[:, None] == vocab_index[None, :]
    picked = jnp.sum(jnp.where(matches, capped, 0.0), axis=1)
    vocab_sums = jnp.stack([totals, picked], axis=0)
    summed_terms = lax.psum(vocab_sums, ("cand", "tensor"))
    own_terms = lax.dynamic_slice_in_dim(summed_terms, cand_id * length, length, 1)
    mask_values = loss_mask.astype(jnp.float32)
    token_loss = mask_values * (jnp.log(own_terms[0]) - own_terms[1])
    onehot = (chosen == jnp.arange(CANDS)).astype(jnp.float32)
    loss_sums, counts = lax.psum(
        (onehot * jnp.sum(token_loss), onehot * jnp.sum(mask_values)), "cand"
    )
    return (token_loss, loss_sums / jnp.maximum(counts, 1.0))


def solution(mesh):
    in_specs = (
        P("cand", None),
        P(),
        P("cand"),
        P(),
        P(),
        P("cand", "tensor"),
        P(None, "cand", "tensor"),
        P("cand", None),
        P(None, "cand", None),
        P("cand", None),
        P(None, "cand", None),
        P("tensor", "cand"),
        P(None, "tensor", "cand"),
        P(),
        P(),
        P(),
        P(None, ("cand", "tensor")),
    )
    out_specs = (P("cand"), P())
    return jax.shard_map(
        on_device, mesh=mesh, in_specs=in_specs, out_specs=out_specs, check_vma=False
    )
```

profile of v0, /device:TPU:0, one launch (start us, length us, event | category | flops | bytes accessed | tf_op | source)
XLA Modules:
  0.0 451.5 jit_solution(439209231556427896)
XLA Ops:
  7.2 0.0 copy-start.2
  7.2 0.0 all-gather.14.cloned.1.call-start
  7.2 1.9 constant_dynamic-slice_fusion.1
  9.2 0.0 all-gather.14.cloned.1.call-update
  9.2 0.0 all-gather.16.cloned.1.call-start
  9.2 2.3 dynamic-slice_reduce_fusion
  11.5 0.0 all-gather.16.cloned.1.call-update
  11.6 0.0 all-gather.20.cloned.1.call-start
  11.6 0.0 copy-done.2
  11.6 1.6 reduce_sum.123
  13.2 0.0 all-gather.20.cloned.1.call-update
  13.2 0.0 all-gather.18.cloned.1.call-start
  13.2 0.5 all-gather.18.cloned.1.call-update
  13.8 0.0 all-gather.10.cloned.1.call-start
  13.8 1.8 constant_dynamic-slice_fusion.2
  15.7 0.0 all-gather.10.cloned.1.call-update
  15.7 0.0 copy-start.8
  15.7 0.0 all-gather.12.cloned.1.call-start
  15.7 2.4 dynamic-slice_reduce_fusion.1
  18.1 0.0 all-gather.12.cloned.1.call-update
  18.2 0.0 all-gather.24.cloned.1.call-start
  18.2 1.5 reduce_sum.125
  19.7 0.0 all-gather.24.cloned.1.call-update
  19.7 0.0 all-gather.22.cloned.1.call-start
  19.8 0.7 all-gather.22.cloned.1.call-update
  20.5 0.0 all-reduce.3.cloned.1.call-start
  20.6 0.6 dynamic_slice.22
  23.1 0.6 dynamic_slice.23
  23.7 0.3 fusion.4
  24.0 0.3 multiply_cosine_fusion
  24.3 9.1 %all-gather.14.cloned.1.call-done = bf16[3584,256]{1,0:T(8,128)(2,1)} async-done(((bf16[896,256]{1,0:T(8,128)(2,1)}), bf16[3584,256]{1,0:T(8,128)(2,1)}) %all-gather.14.cloned.1.call-update) | async-done | bytes 1835024 | tf_op jit(solution)/shard_map/all_gather | solution.py:74
  33.4 22.7 %all-gather.16.cloned.1.call-done = bf16[3584,256]{1,0:T(8,128)(2,1)} async-done(((bf16[896,256]{1,0:T(8,128)(2,1)}), bf16[3584,256]{1,0:T(8,128)(2,1)}) %all-gather.16.cloned.1.call-update) | async-done | bytes 1835024 | tf_op jit(solution)/shard_map/all_gather | solution.py:78
  56.1 0.0 copy-done.8
  56.1 3.6 fusion.20
  59.7 0.3 fusion.37
  60.0 29.2 %all-gather.20.cloned.1.call-done = bf16[3584,512]{1,0:T(8,128)(2,1)} async-done(((bf16[896,512]{1,0:T(8,128)(2,1)}), bf16[3584,512]{1,0:T(8,128)(2,1)}) %all-gather.20.cloned.1.call-update) | async-done | bytes 3670032 | tf_op jit(solution)/shard_map/all_gather | solution.py:77
  89.2 32.9 %all-gather.18.cloned.1.call-done = bf16[3584,512]{1,0:T(8,128)(2,1)} async-done(((bf16[896,512]{1,0:T(8,128)(2,1)}), bf16[3584,512]{1,0:T(8,128)(2,1)}) %all-gather.18.cloned.1.call-update) | async-done | bytes 3670032 | tf_op jit(solution)/shard_map/all_gather | solution.py:73
  122.1 5.2 %fusion = f32[128,512]{1,0:T(8,128)S(1)} fusion(bf16[3584,512]{1,0:T(8,128)(2,1)} %all-gather.20.cloned.1.call-done, bf16[3584,512]{1,0:T(8,128)(2,1)} %all-gather.18.cloned.1.call-done, f32[]{:T(128)} %bitcast.1, bf16[128,3584]{1,0:T(8,128)(2,1)S(1)} %copy-done.1, f32[3584]{0:T(1024)S(1)} %copy-done.8, f32[128]{0:T(128)S(1)} %add_rsqrt_fusion.2), kind=kOutput, calls=%fused_computation.6 | convolution fusion | flops 480772096 | bytes 8534532 | tf_op jit(solution)/shard_map/dot_general | solution.py:91
  127.3 0.2 reshape.177
  127.5 0.1 fusion.53
  127.7 0.2 fusion.15
  127.9 16.7 %all-gather.10.cloned.1.call-done = bf16[3584,256]{1,0:T(8,128)(2,1)} async-done(((bf16[896,256]{1,0:T(8,128)(2,1)}), bf16[3584,256]{1,0:T(8,128)(2,1)}) %all-gather.10.cloned.1.call-update) | async-done | bytes 1835024 | tf_op jit(solution)/shard_map/all_gather | solution.py:75
  144.6 22.5 %all-gather.12.cloned.1.call-done = bf16[3584,256]{1,0:T(8,128)(2,1)} async-done(((bf16[896,256]{1,0:T(8,128)(2,1)}), bf16[3584,256]{1,0:T(8,128)(2,1)}) %all-gather.12.cloned.1.call-update) | async-done | bytes 1835024 | tf_op jit(solution)/shard_map/all_gather | solution.py:79
  167.2 3.9 convolution_convert_fusion
  171.1 29.1 %all-gather.24.cloned.1.call-done = bf16[512,3584]{1,0:T(8,128)(2,1)} async-done(((bf16[512,896]{1,0:T(8,128)(2,1)}), bf16[512,3584]{1,0:T(8,128)(2,1)}) %all-gather.24.cloned.1.call-update) | async-done | bytes 3670032 | tf_op jit(solution)/shard_map/all_gather | solution.py:80
  200.2 33.1 %all-gather.22.cloned.1.call-done = bf16[512,3584]{1,0:T(8,128)(2,1)} async-done(((bf16[512,896]{1,0:T(8,128)(2,1)}), bf16[512,3584]{1,0:T(8,128)(2,1)}) %all-gather.22.cloned.1.call-update) | async-done | bytes 3670032 | tf_op jit(solution)/shard_map/all_gather | solution.py:76
  233.3 6.6 %fusion.1 = f32[128,3584]{1,0:T(8,128)} fusion(bf16[128,512]{0,1:T(8,128)(2,1)S(1)} %bitcast.38, bf16[512,3584]{1,0:T(8,128)(2,1)} %all-gather.24.cloned.1.call-done, bf16[512,3584]{1,0:T(8,128)(2,1)} %all-gather.22.cloned.1.call-done, f32[]{:T(128)} %bitcast.1), kind=kOutput, calls=%fused_computation.7 | convolution fusion | flops 478937088 | bytes 9306116 | tf_op jit(solution)/shard_map/dot_general | solution.py:111
  239.9 0.0 all-reduce.3.cloned.1.call-update
  239.9 0.2 all-gather.26.cloned.1.call-start
  240.2 95.7 %all-reduce.3.cloned.1.call-done = f32[128,3584]{1,0:T(8,128)} async-done(((f32[128,3584]{1,0:T(8,128)}), f32[128,3584]{1,0:T(8,128)}) %all-reduce.3.cloned.1.call-update) | async-done | bytes 1835024 | tf_op jit(solution)/shard_map/psum | solution.py:115
  335.9 1.8 multiply_reduce_fusion.1
  337.8 0.0 copy-done.4
  337.8 0.0 copy-start.6
  337.8 2.0 multiply_reduce_fusion
  339.8 1.4 multiply_convert_fusion
  341.2 0.0 all-gather.26.cloned.1.call-update
  341.3 0.0 copy-start.7
  341.3 31.1 %all-gather.26.cloned.1.call-done = bf16[512,3584]{1,0:T(8,128)(2,1)} async-done(((bf16[128,3584]{1,0:T(8,128)(2,1)}), bf16[512,3584]{1,0:T(8,128)(2,1)}) %all-gather.26.cloned.1.call-update) | async-done | bytes 3670032 | tf_op jit(solution)/shard_map/all_gather | solution.py:118
  372.4 22.9 %exponential_reduce_fusion = (f32[512]{0:T(512)S(1)}, f32[512]{0:T(512)S(1)}) fusion(s32[512]{0:T(512)S(1)} %broadcast_subtract_fusion, bf16[512,3584]{1,0:T(8,128)(2,1)} %all-gather.26.cloned.1.call-done, bf16[3584,4096]{1,0:T(8,128)(2,1)} %param.33), kind=kOutput, calls=%fused_computation.2 | convolution fusion | flops 15044968448 | bytes 33036288 | tf_op jit(solution)/shard_map/dot_general | solution.py:117
  395.3 39.3 %psum.29 = f32[2,512]{1,0:T(2,128)S(1)} all-reduce(f32[2,512]{1,0:T(2,128)S(1)} %pad_maximum_fusion), channel_id=1, replica_groups=mesh['cand'=4,'tensor'=8] {'cand','tensor'}, use_global_device_ids=true, to_apply=%region_11.12 | all-reduce | flops 1024 | bytes 8192 | tf_op jit(solution)/shard_map/psum | solution.py:128
  434.7 1.1 fusion.52
  435.8 1.8 compare_select_fusion
  437.6 6.5 %all-reduce = (f32[4]{0:T(128)S(1)}, f32[4]{0:T(128)S(1)}) all-reduce(f32[4]{0:T(128)S(1)} %get-tuple-element.18, f32[4]{0:T(128)S(1)} %get-tuple-element.17), channel_id=1, replica_groups=mesh['cand'=4,'tensor'=8] {'cand'}, use_global_device_ids=true, to_apply=%region_13.14 | all-reduce | flops 8 | bytes 64 | tf_op jit(solution)/shard_map/psum | solution.py:133
  444.2 0.5 maximum_divide_fusion
  (25 shorter events, 0.1 us)
Async XLA Ops:
  7.2 4.4 copy-start.2
  7.2 26.2 %all-gather.14.cloned.1.call-start = ((), (), s32[]{:S(2)}) async-start(), calls=%async_computation.2 | async-start | bytes 2293760 | tf_op jit(solution)/shard_map/all_gather | solution.py:74
  9.2 46.9 %all-gather.16.cloned.1.call-start = ((), (), s32[]{:S(2)}) async-start(), calls=%async_computation.3 | async-start | bytes 2293760 | tf_op jit(solution)/shard_map/all_gather | solution.py:78
  11.6 77.6 %all-gather.20.cloned.1.call-start = ((), (), s32[]{:S(2)}) async-start(), calls=%async_computation.5 | async-start | bytes 4587520 | tf_op jit(solution)/shard_map/all_gather | solution.py:77
  13.2 5.0 %copy-start.3 = (bf16[2,512,896]{2,1,0:T(8,128)(2,1)S(1)}, bf16[2,512,896]{2,1,0:T(8,128)(2,1)}, u32[]{:S(2)}) copy-start(bf16[2,512,896]{2,1,0:T(8,128)(2,1)} %param.29) | copy-start | bytes 5505028
  13.2 108.9 %all-gather.18.cloned.1.call-start = ((), (), s32[]{:S(2)}) async-start(), calls=%async_computation.4 | async-start | bytes 4587520 | tf_op jit(solution)/shard_map/all_gather | solution.py:73
  13.8 130.9 %all-gather.10.cloned.1.call-start = ((), (), s32[]{:S(2)}) async-start(), calls=%async_computation | async-start | bytes 2293760 | tf_op jit(solution)/shard_map/all_gather | solution.py:75
  15.6 4.9 %copy-start.9 = (s32[4]{0:T(128)S(1)}, s32[4]{0:T(128)}, u32[]{:S(2)}) copy-start(s32[4]{0:T(128)} %param.20) | copy-start | bytes 52
  15.6 7.4 %copy-start.10 = (f32[4]{0:T(128)S(1)}, f32[4]{0:T(128)}, u32[]{:S(2)}) copy-start(f32[4]{0:T(128)} %param.21) | copy-start | bytes 52
  15.7 8.1 %copy-start.1 = (bf16[128,3584]{1,0:T(8,128)(2,1)S(1)}, bf16[128,3584]{1,0:T(8,128)(2,1)}, u32[]{:S(2)}) copy-start(bf16[128,3584]{1,0:T(8,128)(2,1)} %param.17) | copy-start | bytes 2752516
  15.7 40.4 %copy-start.8 = (f32[3584]{0:T(1024)S(1)}, f32[3584]{0:T(1024)}, u32[]{:S(2)}) copy-start(f32[3584]{0:T(1024)} %param.30) | copy-start | bytes 43012
  15.7 151.5 %all-gather.12.cloned.1.call-start = ((), (), s32[]{:S(2)}) async-start(), calls=%async_computation.1 | async-start | bytes 2293760 | tf_op jit(solution)/shard_map/all_gather | solution.py:79
  18.2 182.1 %all-gather.24.cloned.1.call-start = ((), (), s32[]{:S(2)}) async-start(), calls=%async_computation.7 | async-start | bytes 4587520 | tf_op jit(solution)/shard_map/all_gather | solution.py:80
  19.7 213.6 %all-gather.22.cloned.1.call-start = ((), (), s32[]{:S(2)}) async-start(), calls=%async_computation.6 | async-start | bytes 4587520 | tf_op jit(solution)/shard_map/all_gather | solution.py:76
  20.5 315.4 %all-reduce.3.cloned.1.call-start = ((), (), s32[]{:S(2)}) async-start(), calls=%async_computation.8 | async-start | bytes 3670016 | tf_op jit(solution)/shard_map/psum | solution.py:115
  239.9 97.8 %copy-start.4 = (f32[3584]{0:T(1024)S(1)}, f32[3584]{0:T(1024)}, u32[]{:S(2)}) copy-start(f32[3584]{0:T(1024)} %param.31) | copy-start | bytes 43012
  239.9 99.9 %copy-start.5 = (f32[3584]{0:T(1024)S(1)}, f32[3584]{0:T(1024)}, u32[]{:S(2)}) copy-start(f32[3584]{0:T(1024)} %param.32) | copy-start | bytes 43012
  239.9 132.5 %all-gather.26.cloned.1.call-start = ((), (), s32[]{:S(2)}) async-start(), calls=%async_computation.9 | async-start | bytes 4587520 | tf_op jit(solution)/shard_map/all_gather | solution.py:118
  335.9 3.9 copy-start
  337.8 3.5 copy-start.6
  341.3 93.4 %copy-start.7 = (s32[128]{0:T(128)S(1)}, s32[128]{0:T(128)}, u32[]{:S(2)}) copy-start(s32[128]{0:T(128)} %param.19) | copy-start | bytes 1540
Sparse Core Ops, SparseCore 0:
  9.5 23.8 all-gather.13
  35.0 21.0 all-gather.15
  57.7 31.4 all-gather.19
  90.6 31.4 all-gather.17
  123.5 21.0 all-gather.9
  146.1 21.0 all-gather.11
  168.7 31.4 all-gather.23
  201.8 31.4 all-gather.21
  240.1 95.7 all-reduce.2
  341.4 30.9 all-gather.25
where the time goes:
time: 452 us
  waiting for transfers between devices  324 us (72%)
  blocking collectives  45.9 us (10%)
  matrix products  42.5 us (9%)
  other arithmetic  17.5 us (4%)
  between operations  16.3 us (4%)
  local copies, waits for them, and re-layouts  5.26 us (1%)
    psum x1, waiting for transfers between devices, on_device(): attended = lax.psum(partial_value, 'tensor')  95.7 us
    psum x1, blocking collectives, on_device(): summed_terms = lax.psum(vocab_sums, ('cand', 'tensor'))  39.3 us
    all_gather x1, waiting for transfers between devices, on_device(): lax.all_gather(base_o, 'cand', axis=1, tiled=True)  33.1 us
    all_gather x1, waiting for transfers between devices, on_device(): lax.all_gather(base_q, 'cand', axis=0, tiled=True)  32.9 us
    all_gather x1, waiting for transfers between devices, on_device(): lax.all_gather(final_rows, 'cand', axis=0, tiled=True)  31.1 us
    all_gather x1, waiting for transfers between devices, on_device(): lax.all_gather(summed[0], 'cand', axis=0, tiled=True)  29.2 us
    all_gather x1, waiting for transfers between devices, on_device(): lax.all_gather(summed[3], 'cand', axis=1, tiled=True)  29.1 us
    dot_general x1, matrix products, on_device(): jnp.dot(lax.all_gather(final_rows, 'cand', axis=0, tiled=True), unembed,...  22.9 us
  transfers between devices with their start and end apart: 10, of which 10 were waited for; matrix products, arithmetic and copies ran while one was open for 6% of the time, Pallas kernels for 0%

commit v1 on v0

--- a/solution.py
+++ b/solution.py
@@ -112,7 +112,7 @@
     vocab_width = unembed.shape[1]
     vocab_start = (cand_id * tensor_count + tensor_id) * vocab_width
     vocab_index = jnp.arange(vocab_width)
-    attended = lax.psum(partial_value, "tensor")
+    attended = jnp.sum(lax.all_gather(partial_value, "tensor"), axis=0)
     final_rows = root_norm(stream + root_norm(attended, post_gain), final_gain).astype(jnp.bfloat16)
     logits = jnp.dot(
         lax.all_gather(final_rows, "cand", axis=0, tiled=True),

time: 452 us -> 560 us (1.24)
  waiting for transfers between devices: 324 us -> 428 us
    all_gather x0 -> x1, waiting for transfers between devices: none -> 202 us  [on_device(): attended = jnp.sum(lax.all_gather(partial_value, 'tensor'), axis=0)]
    psum x1 -> x0, waiting for transfers between devices: 95.7 us -> none  [on_device(): attended = lax.psum(partial_value, 'tensor')]
    reduce_sum x0 -> x1, other arithmetic: none -> 6.63 us  [on_device(): attended = jnp.sum(lax.all_gather(partial_value, 'tensor'), axis=0)]
  transfers between devices with their start and end apart: 10 -> 10, of which waited for: 10 -> 10; matrix products, arithmetic and copies ran while one was open for 6% -> 4% of each run, Pallas kernels for 0% -> 0%
where the time goes in v1:
time: 560 us
  waiting for transfers between devices  428 us (76%)
  blocking collectives  45.9 us (8%)
  matrix products  42.4 us (8%)
  other arithmetic  21 us (4%)
  between operations  16.3 us (3%)
    all_gather x1, waiting for transfers between devices, on_device(): attended = jnp.sum(lax.all_gather(partial_value, 'tensor'), axis=0)  202 us
    psum x1, blocking collectives, on_device(): summed_terms = lax.psum(vocab_sums, ('cand', 'tensor'))  39.3 us
    all_gather x1, waiting for transfers between devices, on_device(): lax.all_gather(base_o, 'cand', axis=1, tiled=True)  33.1 us
    all_gather x1, waiting for transfers between devices, on_device(): lax.all_gather(base_q, 'cand', axis=0, tiled=True)  32.9 us
    all_gather x1, waiting for transfers between devices, on_device(): lax.all_gather(final_rows, 'cand', axis=0, tiled=True)  29.8 us
    all_gather x1, waiting for transfers between devices, on_device(): lax.all_gather(summed[0], 'cand', axis=0, tiled=True)  29.2 us
    all_gather x1, waiting for transfers between devices, on_device(): lax.all_gather(summed[3], 'cand', axis=1, tiled=True)  29.1 us
    dot_general x1, matrix products, on_device(): jnp.dot(lax.all_gather(final_rows, 'cand', axis=0, tiled=True), unembed,...  22.9 us
  transfers between devices with their start and end apart: 10, of which 10 were waited for; matrix products, arithmetic and copies ran while one was open for 4% of the time, Pallas kernels for 0%

profile of v1, /device:TPU:0, one launch (start us, length us, event | category | flops | bytes accessed | tf_op | source)
XLA Modules:
  0.0 559.5 jit_solution(8946879134665706387)
XLA Ops:
  7.2 0.0 copy-start.1
  7.2 0.0 all-gather.16.cloned.1.call-start
  7.2 1.9 constant_dynamic-slice_fusion.1
  9.2 0.0 all-gather.16.cloned.1.call-update
  9.2 0.0 all-gather.18.cloned.1.call-start
  9.2 2.3 dynamic-slice_reduce_fusion
  11.5 0.0 all-gather.18.cloned.1.call-update
  11.5 0.0 all-gather.22.cloned.1.call-start
  11.6 0.0 copy-done.1
  11.6 1.5 reduce_sum.132
  13.1 0.0 all-gather.22.cloned.1.call-update
  13.2 0.0 all-gather.20.cloned.1.call-start
  13.2 0.5 all-gather.20.cloned.1.call-update
  13.7 0.0 all-gather.12.cloned.1.call-start
  13.8 1.8 constant_dynamic-slice_fusion.2
  15.6 0.0 all-gather.12.cloned.1.call-update
  15.6 0.0 copy-start.7
  15.7 0.0 all-gather.14.cloned.1.call-start
  15.7 2.4 dynamic-slice_reduce_fusion.1
  18.1 0.0 all-gather.14.cloned.1.call-update
  18.1 0.0 all-gather.26.cloned.1.call-start
  18.2 1.5 reduce_sum.134
  19.7 0.0 all-gather.26.cloned.1.call-update
  19.7 0.0 all-gather.24.cloned.1.call-start
  19.7 0.7 all-gather.24.cloned.1.call-update
  20.4 0.0 all-gather.30.cloned.1.call-start
  20.5 0.6 dynamic_slice.22
  23.0 0.6 dynamic_slice.23
  23.7 0.3 fusion.4
  24.0 0.3 multiply_cosine_fusion
  24.3 9.1 %all-gather.16.cloned.1.call-done = bf16[3584,256]{1,0:T(8,128)(2,1)} async-done(((bf16[896,256]{1,0:T(8,128)(2,1)}), bf16[3584,256]{1,0:T(8,128)(2,1)}) %all-gather.16.cloned.1.call-update) | async-done | bytes 1835024 | tf_op jit(solution)/shard_map/all_gather | solution.py:74
  33.4 22.7 %all-gather.18.cloned.1.call-done = bf16[3584,256]{1,0:T(8,128)(2,1)} async-done(((bf16[896,256]{1,0:T(8,128)(2,1)}), bf16[3584,256]{1,0:T(8,128)(2,1)}) %all-gather.18.cloned.1.call-update) | async-done | bytes 1835024 | tf_op jit(solution)/shard_map/all_gather | solution.py:78
  56.1 3.6 fusion.20
  59.7 0.3 fusion.37
  60.0 29.2 %all-gather.22.cloned.1.call-done = bf16[3584,512]{1,0:T(8,128)(2,1)} async-done(((bf16[896,512]{1,0:T(8,128)(2,1)}), bf16[3584,512]{1,0:T(8,128)(2,1)}) %all-gather.22.cloned.1.call-update) | async-done | bytes 3670032 | tf_op jit(solution)/shard_map/all_gather | solution.py:77
  89.2 32.9 %all-gather.20.cloned.1.call-done = bf16[3584,512]{1,0:T(8,128)(2,1)} async-done(((bf16[896,512]{1,0:T(8,128)(2,1)}), bf16[3584,512]{1,0:T(8,128)(2,1)}) %all-gather.20.cloned.1.call-update) | async-done | bytes 3670032 | tf_op jit(solution)/shard_map/all_gather | solution.py:73
  122.1 5.2 fusion
  127.3 0.2 reshape.177
  127.5 0.1 fusion.53
  127.7 0.2 fusion.15
  127.9 16.7 %all-gather.12.cloned.1.call-done = bf16[3584,256]{1,0:T(8,128)(2,1)} async-done(((bf16[896,256]{1,0:T(8,128)(2,1)}), bf16[3584,256]{1,0:T(8,128)(2,1)}) %all-gather.12.cloned.1.call-update) | async-done | bytes 1835024 | tf_op jit(solution)/shard_map/all_gather | solution.py:75
  144.6 22.5 %all-gather.14.cloned.1.call-done = bf16[3584,256]{1,0:T(8,128)(2,1)} async-done(((bf16[896,256]{1,0:T(8,128)(2,1)}), bf16[3584,256]{1,0:T(8,128)(2,1)}) %all-gather.14.cloned.1.call-update) | async-done | bytes 1835024 | tf_op jit(solution)/shard_map/all_gather | solution.py:79
  167.2 3.9 convolution_convert_fusion
  171.1 29.1 %all-gather.26.cloned.1.call-done = bf16[512,3584]{1,0:T(8,128)(2,1)} async-done(((bf16[512,896]{1,0:T(8,128)(2,1)}), bf16[512,3584]{1,0:T(8,128)(2,1)}) %all-gather.26.cloned.1.call-update) | async-done | bytes 3670032 | tf_op jit(solution)/shard_map/all_gather | solution.py:80
  200.2 33.1 %all-gather.24.cloned.1.call-done = bf16[512,3584]{1,0:T(8,128)(2,1)} async-done(((bf16[512,896]{1,0:T(8,128)(2,1)}), bf16[512,3584]{1,0:T(8,128)(2,1)}) %all-gather.24.cloned.1.call-update) | async-done | bytes 3670032 | tf_op jit(solution)/shard_map/all_gather | solution.py:76
  233.3 6.5 %fusion.1 = f32[128,3584]{1,0:T(8,128)} fusion(bf16[128,512]{0,1:T(8,128)(2,1)S(1)} %bitcast.40, bf16[512,3584]{1,0:T(8,128)(2,1)} %all-gather.26.cloned.1.call-done, bf16[512,3584]{1,0:T(8,128)(2,1)} %all-gather.24.cloned.1.call-done, f32[]{:T(128)} %bitcast.1), kind=kOutput, calls=%fused_computation.7 | convolution fusion | flops 478937088 | bytes 9306116 | tf_op jit(solution)/shard_map/dot_general | solution.py:111
  239.8 0.0 all-gather.30.cloned.1.call-update
  239.8 0.2 all-gather.28.cloned.1.call-start
  240.1 201.6 %all-gather.30.cloned.1.call-done = f32[1024,3584]{1,0:T(8,128)} async-done(((f32[128,3584]{1,0:T(8,128)}), f32[1024,3584]{1,0:T(8,128)}) %all-gather.30.cloned.1.call-update) | async-done | bytes 14680080 | tf_op jit(solution)/shard_map/all_gather | solution.py:115
  441.7 6.6 %reduce_sum.135 = f32[128,3584]{1,0:T(8,128)S(1)} reduce(f32[8,128,3584]{2,1,0:T(8,128)} %bitcast.39, f32[]{:T(128)} %constant.50.clone.1), dimensions={0}, to_apply=%region_6.7 | reduce | flops 3211264 | bytes 16515076 | tf_op jit(solution)/shard_map/reduce_sum | solution.py:115
  448.3 0.0 copy-start.4
  448.3 0.2 multiply_reduce_fusion.1
  448.5 0.0 copy-start.5
  448.5 0.5 multiply_reduce_fusion
  449.1 1.4 multiply_convert_fusion
  450.5 0.0 all-gather.28.cloned.1.call-update
  450.5 0.0 copy-start.6
  450.5 29.8 %all-gather.28.cloned.1.call-done = bf16[512,3584]{1,0:T(8,128)(2,1)} async-done(((bf16[128,3584]{1,0:T(8,128)(2,1)}), bf16[512,3584]{1,0:T(8,128)(2,1)}) %all-gather.28.cloned.1.call-update) | async-done | bytes 3670032 | tf_op jit(solution)/shard_map/all_gather | solution.py:118
  480.3 22.9 %exponential_reduce_fusion = (f32[512]{0:T(512)S(1)}, f32[512]{0:T(512)S(1)}) fusion(s32[512]{0:T(512)S(1)} %broadcast_subtract_fusion, bf16[512,3584]{1,0:T(8,128)(2,1)} %all-gather.28.cloned.1.call-done, bf16[3584,4096]{1,0:T(8,128)(2,1)} %param.33), kind=kOutput, calls=%fused_computation.2 | convolution fusion | flops 15044968448 | bytes 33036288 | tf_op jit(solution)/shard_map/dot_general | solution.py:117
  503.2 39.3 %psum.21 = f32[2,512]{1,0:T(2,128)S(1)} all-reduce(f32[2,512]{1,0:T(2,128)S(1)} %pad_maximum_fusion), channel_id=1, replica_groups=mesh['cand'=4,'tensor'=8] {'cand','tensor'}, use_global_device_ids=true, to_apply=%region_11.12 | all-reduce | flops 1024 | bytes 8192 | tf_op jit(solution)/shard_map/psum | solution.py:128
  542.6 1.2 fusion.52
  543.7 1.9 compare_select_fusion
  545.6 6.5 %all-reduce = (f32[4]{0:T(128)S(1)}, f32[4]{0:T(128)S(1)}) all-reduce(f32[4]{0:T(128)S(1)} %get-tuple-element.18, f32[4]{0:T(128)S(1)} %get-tuple-element.17), channel_id=1, replica_groups=mesh['cand'=4,'tensor'=8] {'cand'}, use_global_device_ids=true, to_apply=%region_13.14 | all-reduce | flops 8 | bytes 64 | tf_op jit(solution)/shard_map/psum | solution.py:133
  552.1 0.5 maximum_divide_fusion
  (24 shorter events, 0.1 us)
Async XLA Ops:
  7.2 4.4 copy-start.1
  7.2 26.2 %all-gather.16.cloned.1.call-start = ((), (), s32[]{:S(2)}) async-start(), calls=%async_computation.2 | async-start | bytes 2293760 | tf_op jit(solution)/shard_map/all_gather | solution.py:74
  9.2 46.9 %all-gather.18.cloned.1.call-start = ((), (), s32[]{:S(2)}) async-start(), calls=%async_computation.3 | async-start | bytes 2293760 | tf_op jit(solution)/shard_map/all_gather | solution.py:78
  11.5 77.6 %all-gather.22.cloned.1.call-start = ((), (), s32[]{:S(2)}) async-start(), calls=%async_computation.5 | async-start | bytes 4587520 | tf_op jit(solution)/shard_map/all_gather | solution.py:77
  13.1 5.0 copy-start.2
  13.2 108.9 %all-gather.20.cloned.1.call-start = ((), (), s32[]{:S(2)}) async-start(), calls=%async_computation.4 | async-start | bytes 4587520 | tf_op jit(solution)/shard_map/all_gather | solution.py:73
  13.7 130.9 %all-gather.12.cloned.1.call-start = ((), (), s32[]{:S(2)}) async-start(), calls=%async_computation | async-start | bytes 2293760 | tf_op jit(solution)/shard_map/all_gather | solution.py:75
  15.6 4.9 copy-start.8
  15.6 7.4 %copy-start.9 = (f32[4]{0:T(128)S(1)}, f32[4]{0:T(128)}, u32[]{:S(2)}) copy-start(f32[4]{0:T(128)} %param.21) | copy-start | bytes 52
  15.6 8.1 %copy-start = (bf16[128,3584]{1,0:T(8,128)(2,1)S(1)}, bf16[128,3584]{1,0:T(8,128)(2,1)}, u32[]{:S(2)}) copy-start(bf16[128,3584]{1,0:T(8,128)(2,1)} %param.17) | copy-start | bytes 2752516
  15.6 40.4 %copy-start.7 = (f32[3584]{0:T(1024)S(1)}, f32[3584]{0:T(1024)}, u32[]{:S(2)}) copy-start(f32[3584]{0:T(1024)} %param.30) | copy-start | bytes 43012
  15.7 151.5 %all-gather.14.cloned.1.call-start = ((), (), s32[]{:S(2)}) async-start(), calls=%async_computation.1 | async-start | bytes 2293760 | tf_op jit(solution)/shard_map/all_gather | solution.py:79
  18.1 182.1 %all-gather.26.cloned.1.call-start = ((), (), s32[]{:S(2)}) async-start(), calls=%async_computation.7 | async-start | bytes 4587520 | tf_op jit(solution)/shard_map/all_gather | solution.py:80
  19.7 213.6 %all-gather.24.cloned.1.call-start = ((), (), s32[]{:S(2)}) async-start(), calls=%async_computation.6 | async-start | bytes 4587520 | tf_op jit(solution)/shard_map/all_gather | solution.py:76
  20.4 421.2 %all-gather.30.cloned.1.call-start = ((), (), s32[]{:S(2)}) async-start(), calls=%async_computation.9 | async-start | bytes 16515072 | tf_op jit(solution)/shard_map/all_gather | solution.py:115
  239.8 240.5 %all-gather.28.cloned.1.call-start = ((), (), s32[]{:S(2)}) async-start(), calls=%async_computation.8 | async-start | bytes 4587520 | tf_op jit(solution)/shard_map/all_gather | solution.py:118
  441.7 6.9 %copy-start.3 = (f32[3584]{0:T(1024)S(1)}, f32[3584]{0:T(1024)}, u32[]{:S(2)}) copy-start(f32[3584]{0:T(1024)} %param.31) | copy-start | bytes 43012
  448.3 0.8 copy-start.4
  448.5 2.0 copy-start.5
  450.5 92.1 %copy-start.6 = (s32[128]{0:T(128)S(1)}, s32[128]{0:T(128)}, u32[]{:S(2)}) copy-start(s32[128]{0:T(128)} %param.19) | copy-start | bytes 1540
Sparse Core Ops, SparseCore 0:
  9.5 23.8 all-gather.15
  35.0 21.0 all-gather.17
  57.7 31.4 all-gather.21
  90.6 31.4 all-gather.19
  123.5 21.0 all-gather.11
  146.1 21.0 all-gather.13
  168.7 31.4 all-gather.25
  201.8 31.4 all-gather.23
  240.0 201.6 all-gather.29
  450.6 29.6 all-gather.27
